TPU v7x, 32 devices: a whole 2x2x4 slice. The times are simulated.
32 devices in a mesh: rep: 2 (over x), shard: 16 (over z, y, core).
Axes of the slice: x: 2, y: 2, z: 4, core: 2. Of those that a mesh axis runs over, the one named last changes fastest.
Arguments:
- tokens_x: bfloat16 [8192, 4096], P(('rep', 'shard')), may hold values from -6 to 6
- key_grad: bfloat16 [8192, 1024], P(('rep', 'shard')), may hold values from -0.06591797 to 0.06591797
- left_root: bfloat16 [64, 512, 512], P('shard'), may hold values from -1 to 3
- slot_grads: bfloat16 [64, 512, 512], P('shard'), may hold values from -6 to 6
- right_root: bfloat16 [64, 512, 512], P('shard'), may hold values from -1 to 3
- block_slot: int32 [32], replicated, may hold values from 0 to 63, as said below
Outputs:
- grad_key: float32 [4096, 1024], P('shard')
- update: bfloat16 [512, 32, 512], P('shard')
Inputs may be any that keep to these rules, and one draw needn't show every extreme that they name: `block_slot`: the entries are distinct; slot v is slot v % 4 of shard index v // 4; no shard index holds more than 4 blocks, and some shard index holds exactly 4.
All inputs are finite; a program needn't handle non-finite values.
Results may differ from a plain program's by a relative error of at most 0.006.
Values may be sent and summed in bfloat16 or wider, within the bound.
A program may use at most 128 MiB of HBM per device.

v0:
```python
import jax
import jax.numpy as jnp
from jax import lax
from jax.sharding import PartitionSpec as P


def column_term(features, cotangent):
    return lax.dot_general(
        features, cotangent, (((0,), (0,)), ((), ())), preferred_element_type=jnp.float32
    )


def precondition(left_block, grad_block, right_block):
    left_part = jnp.einsum(
        "sij,sjk->sik", left_block, grad_block, preferred_element_type=jnp.float32
    ).astype(jnp.bfloat16)
    return jnp.einsum(
        "sij,sjk->isk", left_part, right_block, preferred_element_type=jnp.float32
    ).astype(jnp.bfloat16)


def shards(tokens_x, key_grad, left_root, slot_grads, right_root, block_slot):
    n_shard = lax.axis_size("shard")
    n_rep = lax.axis_size("rep")
    own_rows = lax.psum_scatter(
        column_term(tokens_x, key_grad), "shard", scatter_dimension=0, tiled=True
    )
    grad_key = lax.psum(own_rows, "rep")
    slot_count = left_root.shape[0]
    half_slots = slot_count // n_rep
    first_slot = lax.axis_index("rep") * half_slots

    def own_half(values):
        return lax.dynamic_slice_in_dim(values, first_slot, half_slots, 0)

    product = precondition(own_half(left_root), own_half(slot_grads), own_half(right_root))
    received = lax.all_to_all(product, "shard", split_axis=0, concat_axis=1, tiled=True)
    joined = lax.all_gather(received, "rep", axis=1, tiled=True)
    owner = block_slot // slot_count
    within = block_slot % slot_count
    position = (
        within // half_slots * (n_shard * half_slots) + owner * half_slots + within % half_slots
    )
    update = jnp.take(joined, position, axis=1)
    return (grad_key, update)


def solution(mesh):
    return jax.shard_map(
        shards,
        mesh=mesh,
        in_specs=(
            P(("rep", "shard"), None),
            P(("rep", "shard"), None),
            P("shard", None, None),
            P("shard", None, None),
            P("shard", None, None),
            P(),
        ),
        out_specs=(P("shard", None), P("shard", None, None)),
        check_vma=False,
    )
```

profile of v0, /device:TPU:0, one launch (start us, length us, event | category | flops | bytes accessed | tf_op | source)
XLA Modules:
  0.0 247.9 jit_solution(18152596970215478150)
XLA Ops:
  8.0 0.0 copy-start
  8.0 0.0 reduce-scatter.2.cloned.1.call-start
  8.1 1.5 copy-done
  9.6 9.2 %fusion.9 = f32[4096,1024]{1,0:T(8,128)} fusion(bf16[256,4096]{1,0:T(8,128)(2,1)S(1)} %copy-done, bf16[256,1024]{1,0:T(8,128)(2,1)} %param.7), kind=kOutput, calls=%fused_computation.23 | convolution fusion | flops 2147483648 | bytes 19398656 | tf_op jit(solution)/shard_map/dot_general | solution.py:8
  18.8 0.0 reduce-scatter.2.cloned.1.call-update
  18.8 0.0 all-gather.2.cloned.1.call-start
  18.8 4.1 %fusion = bf16[512,2,512]{0,2,1:T(8,128)(2,1)} fusion(bf16[4,512,512]{2,1,0:T(8,128)(2,1)} %param.9, s32[]{:T(128)S(6)} %select_n.37, bf16[4,512,512]{2,1,0:T(8,128)(2,1)} %param.8, bf16[4,512,512]{2,1,0:T(8,128)(2,1)} %param.10), kind=kOutput, calls=%fused_computation.3 | convolution fusion | flops 1074790400 | bytes 4195840 | tf_op jit(solution)/shard_map/sij,sjk->isk/dot_general | solution.py:17
  22.9 2.5 %copy.14 = bf16[512,2,512]{2,1,0:T(2,128)(2,1)S(1)} copy(bf16[512,2,512]{0,2,1:T(8,128)(2,1)} %fusion) | data formatting | bytes 2097152 | tf_op jit(solution)/shard_map/convert_element_type | solution.py:19
  25.4 31.9 %all_to_all.18 = bf16[512,2,512]{2,1,0:T(2,128)(2,1)S(1)} all-to-all(bf16[512,2,512]{2,1,0:T(2,128)(2,1)S(1)} %copy.14), channel_id=1, replica_groups=mesh['rep'=2,'shard'=16] {'shard'}, dimensions={0} | all-to-all | bytes 2097152 | tf_op jit(solution)/shard_map/all_to_all | solution.py:37
  57.3 0.2 copy.15
  57.5 0.0 copy-start.1
  57.5 1.0 copy.16
  58.6 0.0 all-gather.2.cloned.1.call-update
  58.6 0.0 all-reduce.2.cloned.1.call-start
  58.6 140.4 %reduce-scatter.2.cloned.1.call-done = f32[256,1024]{1,0:T(8,128)} async-done(((f32[4096,1024]{1,0:T(8,128)}), f32[256,1024]{1,0:T(8,128)}) %reduce-scatter.2.cloned.1.call-update) | async-done | bytes 1048592 | tf_op jit(solution)/shard_map/reduce_scatter | solution.py:25
  199.0 0.0 all-reduce.2.cloned.1.call-update
  199.0 0.0 copy-done.1
  199.1 0.0 all-gather.2.cloned.1.call-done
  199.1 2.2 gather_fusion
  201.3 0.2 select_bitcast_fusion
  201.5 1.5 copy.17
  203.0 35.1 %all-reduce.2.cloned.1.call-done = f32[256,1024]{1,0:T(8,128)} async-done(((f32[256,1024]{1,0:T(8,128)}), f32[256,1024]{1,0:T(8,128)}) %all-reduce.2.cloned.1.call-update) | async-done | bytes 1048592 | tf_op jit(solution)/shard_map/psum | solution.py:28
  238.2 2.3 copy.20
  (2 shorter events, 0.0 us)
Async XLA Ops:
  8.0 1.6 copy-start
  8.0 191.0 %reduce-scatter.2.cloned.1.call-start = ((), (), s32[]{:S(2)}) async-start(), calls=%async_computation.2 | async-start | bytes 17825792 | tf_op jit(solution)/shard_map/reduce_scatter | solution.py:25
  18.8 180.3 %all-gather.2.cloned.1.call-start = ((), (), s32[]{:S(2)}) async-start(), calls=%async_computation.4 | async-start | bytes 3145728 | tf_op jit(solution)/shard_map/all_gather | solution.py:38
  57.5 141.5 %copy-start.1 = (s32[32]{0:T(128)S(1)}, s32[32]{0:T(128)}, u32[]{:S(2)}) copy-start(s32[32]{0:T(128)} %param.11) | copy-start | bytes 388
  58.6 179.6 %all-reduce.2.cloned.1.call-start = ((), (), s32[]{:S(2)}) async-start(), calls=%async_computation.3 | async-start | bytes 2097152 | tf_op jit(solution)/shard_map/psum | solution.py:28
Sparse Core Ops, SparseCore 0:
  18.9 180.0 reduce-scatter.1
Sparse Core Ops, SparseCore 1:
  58.7 33.3 all-gather.1
  199.1 39.0 all-reduce.1
where the time goes:
time: 248 us
  waiting for transfers between devices  176 us (71%)
  blocking collectives  31.9 us (13%)
  between operations  15.6 us (6%)
  matrix products  13.3 us (5%)
  local copies, waits for them, and re-layouts  11.3 us (5%)
    reduce_scatter x1, waiting for transfers between devices, shards(): lax.psum_scatter(column_term(tokens_x, key_grad), 'shard', scatter_dimens...  140 us
    psum x1, waiting for transfers between devices, shards(): grad_key = lax.psum(own_rows, 'rep')  35.1 us
    all_to_all x1, blocking collectives, shards(): lax.all_to_all(product, 'shard', split_axis=0, concat_axis=1, tiled=True)  31.9 us
    dot_general x1, matrix products, column_term(): lax.dot_general(features, cotangent, (((0,), (0,)), ((), ())), preferred_...  9.16 us
    unnamed x6, local copies, waits for them, and re-layouts  5.4 us
  transfers between devices with their start and end apart: 3, of which 2 were waited for; matrix products, arithmetic and copies ran while one was open for 5% of the time, Pallas kernels for 0%

commit v1 on v0

--- a/solution.py
+++ b/solution.py
@@ -2,6 +2,31 @@
 import jax.numpy as jnp
 from jax import lax
 from jax.sharding import PartitionSpec as P
+
+
+def in_blocks(x, dim, peers):
+    lengths = x.shape
+    pieces = x.reshape(*lengths[:dim], peers, lengths[dim] // peers, *lengths[dim + 1 :])
+    return jnp.moveaxis(pieces, dim, 0)
+
+
+def joined_along(pieces, dim):
+    shape = list(pieces.shape[1:])
+    shape[dim] *= pieces.shape[0]
+    return jnp.moveaxis(pieces, 0, dim).reshape(shape)
+
+
+def sent_to_each(x, axis, split_dim, concat_dim):
+    devices, place = (lax.axis_size(axis), lax.axis_index(axis))
+    blocks = in_blocks(x, split_dim, devices)
+    finished = [blocks[place]]
+    for step in range(1, devices):
+        sent = blocks[(place + step) % devices]
+        finished.append(
+            lax.ppermute(sent, axis, [(i, (i + step) % devices) for i in range(devices)])
+        )
+    blocks = jnp.stack(finished)[(place - jnp.arange(devices)) % devices]
+    return joined_along(blocks, concat_dim)
 
 
 def column_term(features, cotangent):
@@ -34,7 +59,7 @@
         return lax.dynamic_slice_in_dim(values, first_slot, half_slots, 0)
 
     product = precondition(own_half(left_root), own_half(slot_grads), own_half(right_root))
-    received = lax.all_to_all(product, "shard", split_axis=0, concat_axis=1, tiled=True)
+    received = sent_to_each(product, "shard", 0, 1)
     joined = lax.all_gather(received, "rep", axis=1, tiled=True)
     owner = block_slot // slot_count
     within = block_slot % slot_count

time: 248 us -> 248 us (level)
  blocking collectives: 31.9 us -> 0 us
  starting transfers between devices: 0.13 us -> 21.9 us
  waiting for transfers between devices: 176 us -> 186 us
    all_to_all x1 -> x0, blocking collectives: 31.9 us -> none  [shards(): lax.all_to_all(product, 'shard', split_axis=0, concat_axis=1, tiled=True)]
    ppermute x0 -> x15, starting transfers between devices: none -> 21.7 us  [sent_to_each(): lax.ppermute(sent, axis, [(i, (i + step) % devices) for i in range(device...]
    ppermute x0 -> x15, waiting for transfers between devices: none -> 9.69 us  [sent_to_each(): lax.ppermute(sent, axis, [(i, (i + step) % devices) for i in range(device...]
    convert_element_type x1 -> x0, local copies, waits for them, and re-layouts: 2.5 us -> none  [precondition(): return jnp.einsum('sij,sjk->isk', left_part, right_block, preferred_eleme...]
    unnamed x6 -> x20, local copies, waits for them, and re-layouts: 5.4 us -> 5.48 us
  transfers between devices with their start and end apart: 3 -> 18, of which waited for: 2 -> 7; matrix products, arithmetic and copies ran while one was open for 5% -> 4% of each run, Pallas kernels for 0% -> 0%
where the time goes in v1:
time: 248 us
  waiting for transfers between devices  186 us (75%)
  starting transfers between devices  21.9 us (9%)
  between operations  15.9 us (6%)
  matrix products  13.2 us (5%)
  local copies, waits for them, and re-layouts  10.6 us (4%)
    reduce_scatter x1, waiting for transfers between devices, shards(): lax.psum_scatter(column_term(tokens_x, key_grad), 'shard', scatter_dimens...  141 us
    psum x1, waiting for transfers between devices, shards(): grad_key = lax.psum(own_rows, 'rep')  35.1 us
    ppermute x15, starting transfers between devices, sent_to_each(): lax.ppermute(sent, axis, [(i, (i + step) % devices) for i in range(device...  21.7 us
    ppermute x15, waiting for transfers between devices, sent_to_each(): lax.ppermute(sent, axis, [(i, (i + step) % devices) for i in range(device...  9.69 us
    dot_general x1, matrix products, column_term(): lax.dot_general(features, cotangent, (((0,), (0,)), ((), ())), preferred_...  9.16 us
    unnamed x20, local copies, waits for them, and re-layouts  5.48 us
  transfers between devices with their start and end apart: 18, of which 7 were waited for; matrix products, arithmetic and copies ran while one was open for 4% of the time, Pallas kernels for 0%

profile of v1, /device:TPU:0, one launch (start us, length us, event | category | flops | bytes accessed | tf_op | source)
XLA Modules:
  0.0 247.9 jit_solution(5651827824811297885)
XLA Ops:
  8.1 1.5 copy-done
  9.6 9.2 %fusion.10 = f32[4096,1024]{1,0:T(8,128)} fusion(bf16[256,4096]{1,0:T(8,128)(2,1)S(1)} %copy-done, bf16[256,1024]{1,0:T(8,128)(2,1)} %param.7), kind=kOutput, calls=%fused_computation.61 | convolution fusion | flops 2147483648 | bytes 19398656 | tf_op jit(solution)/shard_map/dot_general | solution.py:33
  19.1 4.1 %convolution_convert_fusion = bf16[2,512,512]{1,2,0:T(8,128)(2,1)} fusion(bf16[4,512,512]{2,1,0:T(8,128)(2,1)} %param.9, s32[]{:T(128)S(6)} %select_n.170, bf16[4,512,512]{2,1,0:T(8,128)(2,1)} %param.8, bf16[4,512,512]{2,1,0:T(8,128)(2,1)} %param.10), kind=kOutput, calls=%fused_computation.2 | convolution fusion | flops 1074790400 | bytes 4195840 | tf_op jit(solution)/shard_map/sij,sjk->isk/dot_general | solution.py:42
  23.2 1.4 dynamic-slice_bitcast_fusion
  24.5 0.5 collective-permute-start
  25.1 2.6 %collective-permute-start.1 = (bf16[32,2,512]{2,0,1:T(8,128)(2,1)S(1)}, bf16[32,2,512]{2,0,1:T(8,128)(2,1)S(1)}, u32[]{:S(2)}, u32[]{:S(2)}) collective-permute-start(bf16[32,2,512]{2,0,1:T(8,128)(2,1)S(1)} %get-tuple-element.21), channel_id=1, source_target_pairs={{0,2},{1,3},{2,4},{3,5},{4,6},{5,7},{6,8},{7,9},{8,10},{9,11},{10,... | collective-permute-start | bytes 196616 | tf_op jit(solution)/shard_map/ppermute | solution.py:26
  27.6 2.4 collective-permute-start.2
  30.1 1.6 collective-permute-start.3
  32.0 1.1 collective-permute-start.5
  33.1 4.4 %collective-permute-start.6 = (bf16[32,2,512]{2,0,1:T(8,128)(2,1)S(1)}, bf16[32,2,512]{2,0,1:T(8,128)(2,1)S(1)}, u32[]{:S(2)}, u32[]{:S(2)}) collective-permute-start(bf16[32,2,512]{2,0,1:T(8,128)(2,1)S(1)} %get-tuple-element.16), channel_id=1, source_target_pairs={{0,7},{1,8},{2,9},{3,10},{4,11},{5,12},{6,13},{7,14},{8,15},{9,0},... | collective-permute-start | bytes 196616 | tf_op jit(solution)/shard_map/ppermute | solution.py:26
  37.5 0.4 collective-permute-start.7
  38.3 6.6 %collective-permute-done.4 = bf16[32,2,512]{2,0,1:T(8,128)(2,1)S(1)} collective-permute-done((bf16[32,2,512]{2,0,1:T(8,128)(2,1)S(1)}, bf16[32,2,512]{2,0,1:T(8,128)(2,1)S(1)}, u32[]{:S(2)}, u32[]{:S(2)}) %collective-permute-start.4) | collective-permute-done | bytes 65568 | tf_op jit(solution)/shard_map/ppermute | solution.py:26
  45.0 0.4 collective-permute-start.10
  45.4 1.9 collective-permute-start.11
  47.3 2.2 collective-permute-start.12
  49.5 3.4 %collective-permute-start.13 = (bf16[32,2,512]{2,0,1:T(8,128)(2,1)S(1)}, bf16[32,2,512]{2,0,1:T(8,128)(2,1)S(1)}, u32[]{:S(2)}, u32[]{:S(2)}) collective-permute-start(bf16[32,2,512]{2,0,1:T(8,128)(2,1)S(1)} %get-tuple-element.9), channel_id=1, source_target_pairs={{0,14},{1,15},{2,0},{3,1},{4,2},{5,3},{6,4},{7,5},{8,6},{9,7},{10,... | collective-permute-start | bytes 196616 | tf_op jit(solution)/shard_map/ppermute | solution.py:26
  53.4 2.3 collective-permute-done.13
  55.7 0.4 collective-permute-done.14
  56.2 1.6 gather_fusion
  57.8 141.2 %reduce-scatter.2.cloned.1.call-done = f32[256,1024]{1,0:T(8,128)} async-done(((f32[4096,1024]{1,0:T(8,128)}), f32[256,1024]{1,0:T(8,128)}) %reduce-scatter.2.cloned.1.call-update) | async-done | bytes 1048592 | tf_op jit(solution)/shard_map/reduce_scatter | solution.py:50
  199.1 2.2 gather_fusion.1
  201.5 1.5 copy.9
  203.0 35.1 %all-reduce.2.cloned.1.call-done = f32[256,1024]{1,0:T(8,128)} async-done(((f32[256,1024]{1,0:T(8,128)}), f32[256,1024]{1,0:T(8,128)}) %all-reduce.2.cloned.1.call-update) | async-done | bytes 1048592 | tf_op jit(solution)/shard_map/psum | solution.py:53
  238.1 2.3 copy.26
  (46 shorter events, 1.8 us)
Async XLA Ops:
  8.0 1.6 copy-start
  8.0 191.0 %reduce-scatter.2.cloned.1.call-start = ((), (), s32[]{:S(2)}) async-start(), calls=%async_computation.1 | async-start | bytes 17825792 | tf_op jit(solution)/shard_map/reduce_scatter | solution.py:50
  18.8 180.3 %all-gather.2.cloned.1.call-start = ((), (), s32[]{:S(2)}) async-start(), calls=%async_computation.3 | async-start | bytes 3145728 | tf_op jit(solution)/shard_map/all_gather | solution.py:63
  24.5 7.5 %collective-permute-start = (bf16[32,2,512]{2,0,1:T(8,128)(2,1)S(1)}, bf16[32,2,512]{2,0,1:T(8,128)(2,1)S(1)}, u32[]{:S(2)}, u32[]{:S(2)}) collective-permute-start(bf16[32,2,512]{2,0,1:T(8,128)(2,1)S(1)} %get-tuple-element.22), channel_id=1, source_target_pairs={{0,1},{1,2},{2,3},{3,4},{4,5},{5,6},{6,7},{7,8},{8,9},{9,10},{10,1... | collective-permute-start | bytes 196616 | tf_op jit(solution)/shard_map/ppermute | solution.py:26
  25.1 8.0 %collective-permute-start.1 = (bf16[32,2,512]{2,0,1:T(8,128)(2,1)S(1)}, bf16[32,2,512]{2,0,1:T(8,128)(2,1)S(1)}, u32[]{:S(2)}, u32[]{:S(2)}) collective-permute-start(bf16[32,2,512]{2,0,1:T(8,128)(2,1)S(1)} %get-tuple-element.21), channel_id=1, source_target_pairs={{0,2},{1,3},{2,4},{3,5},{4,6},{5,7},{6,8},{7,9},{8,10},{9,11},{10,... | collective-permute-start | bytes 196616 | tf_op jit(solution)/shard_map/ppermute | solution.py:26
  27.6 9.8 %collective-permute-start.2 = (bf16[32,2,512]{2,0,1:T(8,128)(2,1)S(1)}, bf16[32,2,512]{2,0,1:T(8,128)(2,1)S(1)}, u32[]{:S(2)}, u32[]{:S(2)}) collective-permute-start(bf16[32,2,512]{2,0,1:T(8,128)(2,1)S(1)} %get-tuple-element.20), channel_id=1, source_target_pairs={{0,3},{1,4},{2,5},{3,6},{4,7},{5,8},{6,9},{7,10},{8,11},{9,12},{10... | collective-permute-start | bytes 196616 | tf_op jit(solution)/shard_map/ppermute | solution.py:26
  30.1 7.8 %collective-permute-start.3 = (bf16[32,2,512]{2,0,1:T(8,128)(2,1)S(1)}, bf16[32,2,512]{2,0,1:T(8,128)(2,1)S(1)}, u32[]{:S(2)}, u32[]{:S(2)}) collective-permute-start(bf16[32,2,512]{2,0,1:T(8,128)(2,1)S(1)} %get-tuple-element.19), channel_id=1, source_target_pairs={{0,4},{1,5},{2,6},{3,7},{4,8},{5,9},{6,10},{7,11},{8,12},{9,13},{1... | collective-permute-start | bytes 196616 | tf_op jit(solution)/shard_map/ppermute | solution.py:26
  31.6 13.2 %collective-permute-start.4 = (bf16[32,2,512]{2,0,1:T(8,128)(2,1)S(1)}, bf16[32,2,512]{2,0,1:T(8,128)(2,1)S(1)}, u32[]{:S(2)}, u32[]{:S(2)}) collective-permute-start(bf16[32,2,512]{2,0,1:T(8,128)(2,1)S(1)} %get-tuple-element.18), channel_id=1, source_target_pairs={{0,5},{1,6},{2,7},{3,8},{4,9},{5,10},{6,11},{7,12},{8,13},{9,14},{... | collective-permute-start | bytes 196616 | tf_op jit(solution)/shard_map/ppermute | solution.py:26
  32.0 13.0 %collective-permute-start.5 = (bf16[32,2,512]{2,0,1:T(8,128)(2,1)S(1)}, bf16[32,2,512]{2,0,1:T(8,128)(2,1)S(1)}, u32[]{:S(2)}, u32[]{:S(2)}) collective-permute-start(bf16[32,2,512]{2,0,1:T(8,128)(2,1)S(1)} %get-tuple-element.17), channel_id=1, source_target_pairs={{0,6},{1,7},{2,8},{3,9},{4,10},{5,11},{6,12},{7,13},{8,14},{9,15},... | collective-permute-start | bytes 196616 | tf_op jit(solution)/shard_map/ppermute | solution.py:26
  33.1 12.3 %collective-permute-start.6 = (bf16[32,2,512]{2,0,1:T(8,128)(2,1)S(1)}, bf16[32,2,512]{2,0,1:T(8,128)(2,1)S(1)}, u32[]{:S(2)}, u32[]{:S(2)}) collective-permute-start(bf16[32,2,512]{2,0,1:T(8,128)(2,1)S(1)} %get-tuple-element.16), channel_id=1, source_target_pairs={{0,7},{1,8},{2,9},{3,10},{4,11},{5,12},{6,13},{7,14},{8,15},{9,0},... | collective-permute-start | bytes 196616 | tf_op jit(solution)/shard_map/ppermute | solution.py:26
  37.5 9.8 %collective-permute-start.7 = (bf16[32,2,512]{2,0,1:T(8,128)(2,1)S(1)}, bf16[32,2,512]{2,0,1:T(8,128)(2,1)S(1)}, u32[]{:S(2)}, u32[]{:S(2)}) collective-permute-start(bf16[32,2,512]{2,0,1:T(8,128)(2,1)S(1)} %get-tuple-element.15), channel_id=1, source_target_pairs={{0,8},{1,9},{2,10},{3,11},{4,12},{5,13},{6,14},{7,15},{8,0},{9,1},... | collective-permute-start | bytes 196616 | tf_op jit(solution)/shard_map/ppermute | solution.py:26
  37.9 11.6 %collective-permute-start.8 = (bf16[32,2,512]{2,0,1:T(8,128)(2,1)S(1)}, bf16[32,2,512]{2,0,1:T(8,128)(2,1)S(1)}, u32[]{:S(2)}, u32[]{:S(2)}) collective-permute-start(bf16[32,2,512]{2,0,1:T(8,128)(2,1)S(1)} %get-tuple-element.14), channel_id=1, source_target_pairs={{0,9},{1,10},{2,11},{3,12},{4,13},{5,14},{6,15},{7,0},{8,1},{9,2},... | collective-permute-start | bytes 196616 | tf_op jit(solution)/shard_map/ppermute | solution.py:26
  44.8 8.1 %collective-permute-start.9 = (bf16[32,2,512]{2,0,1:T(8,128)(2,1)S(1)}, bf16[32,2,512]{2,0,1:T(8,128)(2,1)S(1)}, u32[]{:S(2)}, u32[]{:S(2)}) collective-permute-start(bf16[32,2,512]{2,0,1:T(8,128)(2,1)S(1)} %get-tuple-element.13), channel_id=1, source_target_pairs={{0,10},{1,11},{2,12},{3,13},{4,14},{5,15},{6,0},{7,1},{8,2},{9,3},... | collective-permute-start | bytes 196616 | tf_op jit(solution)/shard_map/ppermute | solution.py:26
  45.0 8.3 %collective-permute-start.10 = (bf16[32,2,512]{2,0,1:T(8,128)(2,1)S(1)}, bf16[32,2,512]{2,0,1:T(8,128)(2,1)S(1)}, u32[]{:S(2)}, u32[]{:S(2)}) collective-permute-start(bf16[32,2,512]{2,0,1:T(8,128)(2,1)S(1)} %get-tuple-element.12), channel_id=1, source_target_pairs={{0,11},{1,12},{2,13},{3,14},{4,15},{5,0},{6,1},{7,2},{8,3},{9,4},{... | collective-permute-start | bytes 196616 | tf_op jit(solution)/shard_map/ppermute | solution.py:26
  45.4 7.9 %collective-permute-start.11 = (bf16[32,2,512]{2,0,1:T(8,128)(2,1)S(1)}, bf16[32,2,512]{2,0,1:T(8,128)(2,1)S(1)}, u32[]{:S(2)}, u32[]{:S(2)}) collective-permute-start(bf16[32,2,512]{2,0,1:T(8,128)(2,1)S(1)} %get-tuple-element.11), channel_id=1, source_target_pairs={{0,12},{1,13},{2,14},{3,15},{4,0},{5,1},{6,2},{7,3},{8,4},{9,5},{1... | collective-permute-start | bytes 196616 | tf_op jit(solution)/shard_map/ppermute | solution.py:26
  47.3 6.1 %collective-permute-start.12 = (bf16[32,2,512]{2,0,1:T(8,128)(2,1)S(1)}, bf16[32,2,512]{2,0,1:T(8,128)(2,1)S(1)}, u32[]{:S(2)}, u32[]{:S(2)}) collective-permute-start(bf16[32,2,512]{2,0,1:T(8,128)(2,1)S(1)} %get-tuple-element.10), channel_id=1, source_target_pairs={{0,13},{1,14},{2,15},{3,0},{4,1},{5,2},{6,3},{7,4},{8,5},{9,6},{10... | collective-permute-start | bytes 196616 | tf_op jit(solution)/shard_map/ppermute | solution.py:26
  49.5 6.2 %collective-permute-start.13 = (bf16[32,2,512]{2,0,1:T(8,128)(2,1)S(1)}, bf16[32,2,512]{2,0,1:T(8,128)(2,1)S(1)}, u32[]{:S(2)}, u32[]{:S(2)}) collective-permute-start(bf16[32,2,512]{2,0,1:T(8,128)(2,1)S(1)} %get-tuple-element.9), channel_id=1, source_target_pairs={{0,14},{1,15},{2,0},{3,1},{4,2},{5,3},{6,4},{7,5},{8,6},{9,7},{10,... | collective-permute-start | bytes 196616 | tf_op jit(solution)/shard_map/ppermute | solution.py:26
  52.9 3.2 %collective-permute-start.14 = (bf16[32,2,512]{2,0,1:T(8,128)(2,1)S(1)}, bf16[32,2,512]{2,0,1:T(8,128)(2,1)S(1)}, u32[]{:S(2)}, u32[]{:S(2)}) collective-permute-start(bf16[32,2,512]{2,0,1:T(8,128)(2,1)S(1)} %get-tuple-element.8), channel_id=1, source_target_pairs={{0,15},{1,0},{2,1},{3,2},{4,3},{5,4},{6,5},{7,6},{8,7},{9,8},{10,9... | collective-permute-start | bytes 196616 | tf_op jit(solution)/shard_map/ppermute | solution.py:26
  56.2 142.9 %copy-start.1 = (s32[32]{0:T(128)S(1)}, s32[32]{0:T(128)}, u32[]{:S(2)}) copy-start(s32[32]{0:T(128)} %param.11) | copy-start | bytes 388
  57.8 180.4 %all-reduce.2.cloned.1.call-start = ((), (), s32[]{:S(2)}) async-start(), calls=%async_computation.2 | async-start | bytes 2097152 | tf_op jit(solution)/shard_map/psum | solution.py:53
Sparse Core Ops, SparseCore 0:
  18.9 180.0 reduce-scatter.1
Sparse Core Ops, SparseCore 1:
  57.9 34.2 all-gather.1
  199.1 39.0 all-reduce.1
